TPU v7x, 32 devices: a whole 2x2x4 slice. The times are simulated.
32 devices in a mesh: dp: 16 (over z, x, core), ens: 2 (over y).
Axes of the slice: x: 2, y: 2, z: 4, core: 2. Of those that a mesh axis runs over, the one named last changes fastest.
Arguments:
- embeddings: bfloat16 [12288, 1024], P('dp'), may hold values from -6 to 6
- valid_mask: int32 [12288], P('dp'), may hold values 0 or 1
- first_weight: bfloat16 [2, 1024, 4096], P(None, 'dp', 'ens'), may hold values from -0.1875 to 0.1875
- second_weight: bfloat16 [2, 4096, 128], P(None, 'ens'), may hold values from -0.09375 to 0.09375
- thresholds: int32 [2], replicated, may hold values from -256 to 256
Outputs:
- mean_logits: float32 [12288, 128], P('dp')
- kept_share: float32 [2], P('ens')
- agree_share: float32 [2], P('ens')
All inputs are finite; a program needn't handle non-finite values. No bound on the sum of `valid_mask` on one device may be relied on, other than what follows from the above.
Results may differ from a plain program's by a relative error of at most 0.0044.
Values may be sent and summed in bfloat16 or wider, within the bound.
A program may use at most 64 MiB of HBM per device.

v0:
```python
import jax
import jax.numpy as jnp
from jax import lax
from jax.sharding import PartitionSpec as P


def on_device(embeddings, valid_mask, first_weight, second_weight, thresholds):
    member = lax.axis_index("ens")
    own_first = lax.all_to_all(first_weight, "ens", split_axis=0, concat_axis=2, tiled=True)
    own_second = lax.all_to_all(second_weight, "ens", split_axis=0, concat_axis=1, tiled=True)
    full_first = lax.all_gather(own_first[0], "dp", axis=0, tiled=True)
    hidden = jnp.maximum(
        jnp.dot(embeddings, full_first, preferred_element_type=jnp.float32), 0.0
    ).astype(jnp.bfloat16)
    logits_own = jnp.dot(hidden, own_second[0], preferred_element_type=jnp.float32)
    classes = logits_own.shape[1]
    levels = jnp.arange(classes, dtype=jnp.float32)
    grades = (2.0 * levels / (classes - 1) - 1.0) * jnp.sqrt(jnp.float32(3.0 / classes))
    scores = jnp.dot(logits_own, grades, precision=lax.Precision.HIGHEST)
    cutoffs = thresholds.astype(jnp.float32) / 256.0
    own_cutoff = lax.dynamic_index_in_dim(cutoffs, member, 0, keepdims=False)
    validity = valid_mask.astype(jnp.float32)
    kept_soft = validity * jax.nn.sigmoid(4.0 * (scores - own_cutoff))
    kept_total = lax.psum(jnp.sum(kept_soft), "dp")
    mean_logits = lax.psum(logits_own, "ens") / first_weight.shape[0]
    ens_score = jnp.dot(mean_logits, grades, precision=lax.Precision.HIGHEST)
    ens_kept = jax.nn.sigmoid(4.0 * (ens_score - jnp.mean(cutoffs)))
    agree_local = jnp.sum(kept_soft * ens_kept)
    agree_total = lax.psum(agree_local, "dp")
    shard_docs = embeddings.shape[0]
    return (
        mean_logits,
        (kept_total / shard_docs).reshape(1),
        (agree_total / shard_docs).reshape(1),
    )


def solution(mesh):
    return jax.shard_map(
        on_device,
        mesh=mesh,
        in_specs=(P("dp", None), P("dp"), P(None, "dp", "ens"), P(None, "ens", None), P()),
        out_specs=(P("dp", None), P("ens"), P("ens")),
        check_vma=False,
    )
```

profile of v0, /device:TPU:0, one launch (start us, length us, event | category | flops | bytes accessed | tf_op | source)
XLA Modules:
  0.0 184.1 jit_solution(3838105246013471597)
XLA Ops:
  7.2 0.0 copy-start
  7.2 0.0 all-gather.2.cloned.1.call-start
  7.2 13.1 %all_to_all.24 = bf16[2,64,2048]{2,1,0:T(8,128)(2,1)S(1)} all-to-all(bf16[2,64,2048]{2,1,0:T(8,128)(2,1)} %param.7), channel_id=1, replica_groups=mesh['dp'=16,'ens'=2] {'ens'}, dimensions={0} | all-to-all | bytes 1048576 | tf_op jit(solution)/shard_map/all_to_all | solution.py:9
  20.4 0.5 copy.8
  20.9 1.0 copy.9
  21.9 0.0 all-gather.2.cloned.1.call-update
  21.9 16.9 %all_to_all.25 = bf16[2,2048,128]{2,1,0:T(8,128)(2,1)S(1)} all-to-all(bf16[2,2048,128]{2,1,0:T(8,128)(2,1)} %param.8), channel_id=1, replica_groups=mesh['dp'=16,'ens'=2] {'ens'}, dimensions={0} | all-to-all | bytes 2097152 | tf_op jit(solution)/shard_map/all_to_all | solution.py:10
  38.8 58.1 %all-gather.2.cloned.1.call-done = bf16[1024,4096]{1,0:T(8,128)(2,1)} async-done(((bf16[64,4096]{1,0:T(8,128)(2,1)}), bf16[1024,4096]{1,0:T(8,128)(2,1)}) %all-gather.2.cloned.1.call-update) | async-done | bytes 8388624 | tf_op jit(solution)/shard_map/all_gather | solution.py:11
  96.9 0.0 copy-done
  96.9 0.0 copy-start.4
  96.9 0.0 copy-start.3
  96.9 11.8 %fusion = f32[768,128]{1,0:T(8,128)S(1)} fusion(bf16[4096,128]{1,0:T(8,128)(2,1)S(1)} %bitcast.24, bf16[768,1024]{1,0:T(8,128)(2,1)S(1)} %copy-done, bf16[1024,4096]{1,0:T(8,128)(2,1)} %all-gather.2.cloned.1.call-done), kind=kOutput, calls=%fused_computation.1 | convolution fusion | flops 7254048768 | bytes 11403264 | tf_op jit(solution)/shard_map/dot_general | solution.py:15
  108.7 0.0 copy-start.1
  108.7 0.5 convolution_reduce_fusion.1
  109.2 0.0 all-reduce.3.cloned.1.call-start
  109.2 0.2 copy-done.1
  109.5 0.5 all-reduce.3.cloned.1.call-update
  109.9 0.0 copy-done.4
  110.0 0.6 convert_multiply_fusion
  111.2 0.6 dynamic_slice.4
  111.8 25.5 %all-reduce.3.cloned.1.call-done = f32[768,128]{1,0:T(8,128)} async-done(((f32[768,128]{1,0:T(8,128)}), f32[768,128]{1,0:T(8,128)}) %all-reduce.3.cloned.1.call-update) | async-done | bytes 393232 | tf_op jit(solution)/shard_map/psum | solution.py:25
  137.3 1.0 broadcast_multiply_fusion
  138.3 0.0 copy-start.2
  138.3 0.5 convolution_reduce_fusion
  138.8 0.0 copy-done.3
  138.8 1.3 multiply_reduce_fusion
  140.1 33.6 %all-reduce = (f32[]{:T(128)}, f32[]{:T(128)}) all-reduce(f32[]{:T(128)} %get-tuple-element.4, f32[]{:T(128)} %get-tuple-element.3), channel_id=1, replica_groups=mesh['dp'=16,'ens'=2] {'dp'}, use_global_device_ids=true, to_apply=%region_2.3 | all-reduce | flops 2 | bytes 16 | tf_op jit(solution)/shard_map/psum | solution.py:24
  175.0 0.0 copy-done.2
Async XLA Ops:
  7.2 89.7 %copy-start = (bf16[768,1024]{1,0:T(8,128)(2,1)S(1)}, bf16[768,1024]{1,0:T(8,128)(2,1)}, u32[]{:S(2)}) copy-start(bf16[768,1024]{1,0:T(8,128)(2,1)} %param.5) | copy-start | bytes 4718596
  7.2 89.7 %all-gather.2.cloned.1.call-start = ((), (), s32[]{:S(2)}) async-start(), calls=%async_computation.2 | async-start | bytes 8912896 | tf_op jit(solution)/shard_map/all_gather | solution.py:11
  96.9 13.1 %copy-start.4 = (s32[2]{0:T(128)S(1)}, s32[2]{0:T(128)}, u32[]{:S(2)}) copy-start(s32[2]{0:T(128)} %param.9) | copy-start | bytes 28
  96.9 41.9 %copy-start.3 = (s32[768]{0:T(1024)S(1)}, s32[768]{0:T(1024)}, u32[]{:S(2)}) copy-start(s32[768]{0:T(1024)} %param.6) | copy-start | bytes 9220
  108.7 0.8 copy-start.1
  109.2 28.1 %all-reduce.3.cloned.1.call-start = ((), (), s32[]{:S(2)}) async-start(), calls=%async_computation.3 | async-start | bytes 786432 | tf_op jit(solution)/shard_map/psum | solution.py:25
  138.3 36.7 %copy-start.2 = (f32[768,128]{1,0:T(8,128)}, f32[768,128]{1,0:T(8,128)S(1)}, u32[]{:S(2)}) copy-start(f32[768,128]{1,0:T(8,128)S(1)} %broadcast_multiply_fusion) | copy-start | bytes 1179652
Sparse Core Ops, SparseCore 0:
  22.1 74.7 all-gather.1
  112.9 24.3 all-reduce.2
where the time goes:
time: 184 us
  waiting for transfers between devices  84 us (46%)
  blocking collectives  63.6 us (35%)
  between operations  18.2 us (10%)
  matrix products  12.7 us (7%)
  other arithmetic  2.97 us (2%)
  local copies, waits for them, and re-layouts  2.4 us (1%)
    all_gather x1, waiting for transfers between devices, on_device(): full_first = lax.all_gather(own_first[0], 'dp', axis=0, tiled=True)  58.1 us
    psum x1, blocking collectives, on_device(): kept_total = lax.psum(jnp.sum(kept_soft), 'dp')  33.6 us
    psum x1, waiting for transfers between devices, on_device(): mean_logits = lax.psum(logits_own, 'ens') / first_weight.shape[0]  25.5 us
    all_to_all x1, blocking collectives, on_device(): lax.all_to_all(second_weight, 'ens', split_axis=0, concat_axis=1, tiled=T...  16.9 us
    all_to_all x1, blocking collectives, on_device(): lax.all_to_all(first_weight, 'ens', split_axis=0, concat_axis=2, tiled=True)  13.1 us
    dot_general x1, matrix products, on_device(): jnp.dot(hidden, own_second[0], preferred_element_type=jnp.float32)  11.8 us
  transfers between devices with their start and end apart: 2, of which 2 were waited for; matrix products, arithmetic and copies ran while one was open for 1% of the time, Pallas kernels for 0%

commit v1 on v0

--- a/solution.py
+++ b/solution.py
@@ -1,7 +1,16 @@
+import functools
 import jax
 import jax.numpy as jnp
 from jax import lax
 from jax.sharding import PartitionSpec as P
+
+
+def _lay_shifts_all(own_rows, link_axis):
+    front = lax.all_gather(own_rows, link_axis)
+    return jnp.sum(front, 0)
+
+
+read_scenes = functools.partial(_lay_shifts_all, link_axis="ens")
 
 
 def on_device(embeddings, valid_mask, first_weight, second_weight, thresholds):
@@ -22,7 +31,7 @@
     validity = valid_mask.astype(jnp.float32)
     kept_soft = validity * jax.nn.sigmoid(4.0 * (scores - own_cutoff))
     kept_total = lax.psum(jnp.sum(kept_soft), "dp")
-    mean_logits = lax.psum(logits_own, "ens") / first_weight.shape[0]
+    mean_logits = read_scenes(logits_own) / first_weight.shape[0]
     ens_score = jnp.dot(mean_logits, grades, precision=lax.Precision.HIGHEST)
     ens_kept = jax.nn.sigmoid(4.0 * (ens_score - jnp.mean(cutoffs)))
     agree_local = jnp.sum(kept_soft * ens_kept)

time: 184 us -> 165 us (0.90)
  waiting for transfers between devices: 84 us -> 68.9 us
  blocking collectives: 63.6 us -> 56.1 us
  starting transfers between devices: 0.08 us -> 3.63 us
    psum x1 -> x0, waiting for transfers between devices: 25.5 us -> none  [on_device(): mean_logits = lax.psum(logits_own, 'ens') / first_weight.shape[0]]
    all_to_all x1 -> x0, blocking collectives: 16.9 us -> none  [on_device(): lax.all_to_all(second_weight, 'ens', split_axis=0, concat_axis=1, tiled=T...]
    all_gather x0 -> x1, blocking collectives: none -> 11.9 us  [_lay_shifts_all(): front = lax.all_gather(own_rows, link_axis)]
    all_to_all x0 -> x1, waiting for transfers between devices: none -> 10.8 us  [on_device(): lax.all_to_all(second_weight, 'ens', split_axis=0, concat_axis=1, tiled=T...]
    all_to_all x0 -> x1, starting transfers between devices: none -> 3.59 us  [on_device(): lax.all_to_all(second_weight, 'ens', split_axis=0, concat_axis=1, tiled=T...]
    psum x1, blocking collectives: 33.6 us -> 31 us  [on_device(): kept_total = lax.psum(jnp.sum(kept_soft), 'dp')]
where the time goes in v1:
time: 165 us
  waiting for transfers between devices  68.9 us (42%)
  blocking collectives  56.1 us (34%)
  between operations  18.2 us (11%)
  matrix products  12.9 us (8%)
  starting transfers between devices  3.63 us (2%)
  other arithmetic  2.69 us (2%)
  local copies, waits for them, and re-layouts  2.11 us (1%)
    all_gather x1, waiting for transfers between devices, on_device(): full_first = lax.all_gather(own_first[0], 'dp', axis=0, tiled=True)  58.1 us
    psum x1, blocking collectives, on_device(): kept_total = lax.psum(jnp.sum(kept_soft), 'dp')  31 us
    all_to_all x1, blocking collectives, on_device(): lax.all_to_all(first_weight, 'ens', split_axis=0, concat_axis=2, tiled=True)  13.1 us
    dot_general x1, matrix products, on_device(): jnp.dot(hidden, own_second[0], preferred_element_type=jnp.float32)  12 us
    all_gather x1, blocking collectives, _lay_shifts_all(): front = lax.all_gather(own_rows, link_axis)  11.9 us
    all_to_all x1, waiting for transfers between devices, on_device(): lax.all_to_all(second_weight, 'ens', split_axis=0, concat_axis=1, tiled=T...  10.8 us
    all_to_all x1, starting transfers between devices, on_device(): lax.all_to_all(second_weight, 'ens', split_axis=0, concat_axis=1, tiled=T...  3.59 us
  transfers between devices with their start and end apart: 2, of which 2 were waited for; matrix products, arithmetic and copies ran while one was open for 1% of the time, Pallas kernels for 0%

profile of v1, /device:TPU:0, one launch (start us, length us, event | category | flops | bytes accessed | tf_op | source)
XLA Modules:
  0.0 164.5 jit_solution(10188686120547166466)
XLA Ops:
  7.2 0.0 copy-start
  7.2 0.0 all-gather.3.cloned.1.call-start
  7.2 13.1 %all_to_all.24 = bf16[2,64,2048]{2,1,0:T(8,128)(2,1)S(1)} all-to-all(bf16[2,64,2048]{2,1,0:T(8,128)(2,1)} %param.7), channel_id=1, replica_groups=mesh['dp'=16,'ens'=2] {'ens'}, dimensions={0} | all-to-all | bytes 1048576 | tf_op jit(solution)/shard_map/all_to_all | solution.py:18
  20.4 0.5 copy.8
  20.9 1.0 copy.9
  21.9 0.0 all-gather.3.cloned.1.call-update
  21.9 3.6 %all-to-all-start.1 = ((bf16[2,2048,128]{2,1,0:T(8,128)(2,1)}), bf16[2,2048,128]{2,1,0:T(8,128)(2,1)S(1)}, u32[]{:S(2)}, u32[]{:S(2)}) async-start(bf16[2,2048,128]{2,1,0:T(8,128)(2,1)} %param.8), calls=%async_computation.1 | async-start | bytes 2097152 | tf_op jit(solution)/shard_map/all_to_all | solution.py:19
  25.5 1.3 convert_multiply_fusion
  27.4 0.6 dynamic_slice.4
  28.0 10.8 %all-to-all-done.1 = bf16[2,2048,128]{2,1,0:T(8,128)(2,1)S(1)} async-done(((bf16[2,2048,128]{2,1,0:T(8,128)(2,1)}), bf16[2,2048,128]{2,1,0:T(8,128)(2,1)S(1)}, u32[]{:S(2)}, u32[]{:S(2)}) %all-to-all-start.1) | async-done | bytes 1048608 | tf_op jit(solution)/shard_map/all_to_all | solution.py:19
  38.8 0.0 copy-start.2
  38.8 58.1 %all-gather.3.cloned.1.call-done = bf16[1024,4096]{1,0:T(8,128)(2,1)} async-done(((bf16[64,4096]{1,0:T(8,128)(2,1)}), bf16[1024,4096]{1,0:T(8,128)(2,1)}) %all-gather.3.cloned.1.call-update) | async-done | bytes 8388624 | tf_op jit(solution)/shard_map/all_gather | solution.py:20
  96.8 0.0 copy-done.2
  96.8 0.0 copy-done
  96.8 0.0 copy-start.3
  96.8 12.0 %fusion = f32[768,128]{1,0:T(8,128)S(1)} fusion(bf16[4096,128]{1,0:T(8,128)(2,1)} %bitcast.26, bf16[768,1024]{1,0:T(8,128)(2,1)S(1)} %copy-done, bf16[1024,4096]{1,0:T(8,128)(2,1)} %all-gather.3.cloned.1.call-done), kind=kOutput, calls=%fused_computation.1 | convolution fusion | flops 7254048768 | bytes 11403264 | tf_op jit(solution)/shard_map/dot_general | solution.py:24
  108.9 0.5 convolution_reduce_fusion.1
  109.3 11.9 %all-gather = f32[1536,128]{1,0:T(8,128)S(1)} all-gather(f32[768,128]{1,0:T(8,128)S(1)} %fusion), channel_id=2, replica_groups=mesh['dp'=16,'ens'=2] {'ens'}, dimensions={0}, use_global_device_ids=true | all-gather | bytes 1179648 | tf_op jit(solution)/shard_map/all_gather | solution.py:9
  121.3 0.1 reduce_sum.36
  121.4 0.0 copy-start.1
  121.4 0.5 convolution_reduce_fusion
  121.8 0.0 copy-done.3
  121.8 1.3 multiply_reduce_fusion
  123.2 31.0 %all-reduce = (f32[]{:T(128)}, f32[]{:T(128)}) all-reduce(f32[]{:T(128)} %get-tuple-element.4, f32[]{:T(128)} %get-tuple-element.3), channel_id=1, replica_groups=mesh['dp'=16,'ens'=2] {'dp'}, use_global_device_ids=true, to_apply=%region_2.3 | all-reduce | flops 2 | bytes 16 | tf_op jit(solution)/shard_map/psum | solution.py:33
  155.4 0.0 copy-done.1
  (1 shorter events, 0.0 us)
Async XLA Ops:
  7.2 89.7 %copy-start = (bf16[768,1024]{1,0:T(8,128)(2,1)S(1)}, bf16[768,1024]{1,0:T(8,128)(2,1)}, u32[]{:S(2)}) copy-start(bf16[768,1024]{1,0:T(8,128)(2,1)} %param.5) | copy-start | bytes 4718596
  7.2 89.7 %all-gather.3.cloned.1.call-start = ((), (), s32[]{:S(2)}) async-start(), calls=%async_computation.2 | async-start | bytes 8912896 | tf_op jit(solution)/shard_map/all_gather | solution.py:20
  21.9 16.9 %all-to-all-start.1 = ((bf16[2,2048,128]{2,1,0:T(8,128)(2,1)}), bf16[2,2048,128]{2,1,0:T(8,128)(2,1)S(1)}, u32[]{:S(2)}, u32[]{:S(2)}) async-start(bf16[2,2048,128]{2,1,0:T(8,128)(2,1)} %param.8), calls=%async_computation.1 | async-start | bytes 2097152 | tf_op jit(solution)/shard_map/all_to_all | solution.py:19
  38.8 58.1 %copy-start.2 = (bf16[2,2048,128]{2,1,0:T(8,128)(2,1)}, bf16[2,2048,128]{2,1,0:T(8,128)(2,1)S(1)}, u32[]{:S(2)}) copy-start(bf16[2,2048,128]{2,1,0:T(8,128)(2,1)S(1)} %all-to-all-done.1) | copy-start | bytes 3145732
  96.8 25.0 %copy-start.3 = (s32[768]{0:T(1024)S(1)}, s32[768]{0:T(1024)}, u32[]{:S(2)}) copy-start(s32[768]{0:T(1024)} %param.6) | copy-start | bytes 9220
  121.4 34.0 %copy-start.1 = (f32[768,128]{1,0:T(8,128)}, f32[768,128]{1,0:T(8,128)S(1)}, u32[]{:S(2)}) copy-start(f32[768,128]{1,0:T(8,128)S(1)} %broadcast_multiply_fusion) | copy-start | bytes 1179652
Sparse Core Ops, SparseCore 0:
  22.0 74.7 all-gather.2

commit v2 on v0

--- a/solution.py
+++ b/solution.py
@@ -4,9 +4,15 @@
 from jax.sharding import PartitionSpec as P
 
 
+def stacked_exchange(x, axis, split, join):
+    pieces = jnp.split(x, lax.axis_size(axis), axis=split)
+    received = lax.all_to_all(jnp.stack(pieces), axis, 0, 0)
+    return jnp.concatenate(received, axis=join)
+
+
 def on_device(embeddings, valid_mask, first_weight, second_weight, thresholds):
     member = lax.axis_index("ens")
-    own_first = lax.all_to_all(first_weight, "ens", split_axis=0, concat_axis=2, tiled=True)
+    own_first = stacked_exchange(first_weight, "ens", 0, 2)
     own_second = lax.all_to_all(second_weight, "ens", split_axis=0, concat_axis=1, tiled=True)
     full_first = lax.all_gather(own_first[0], "dp", axis=0, tiled=True)
     hidden = jnp.maximum(

time: 184 us -> 188 us (1.022)
  matrix products: 12.7 us -> 15.8 us
    dot_general x1, matrix products: 11.8 us -> 14.9 us  [on_device(): jnp.dot(hidden, own_second[0], preferred_element_type=jnp.float32)]
where the time goes in v2:
time: 188 us; the launch traced here: 187 us
  waiting for transfers between devices  84.5 us (45%)
  blocking collectives  62 us (33%)
  between operations  18.3 us (10%)
  matrix products  15.8 us (8%)
  local copies, waits for them, and re-layouts  3.57 us (2%)
  other arithmetic  3.02 us (2%)
    all_gather x1, waiting for transfers between devices, on_device(): full_first = lax.all_gather(own_first[0], 'dp', axis=0, tiled=True)  58.5 us
    psum x1, blocking collectives, on_device(): kept_total = lax.psum(jnp.sum(kept_soft), 'dp')  33.6 us
    psum x1, waiting for transfers between devices, on_device(): mean_logits = lax.psum(logits_own, 'ens') / first_weight.shape[0]  25.5 us
    all_to_all x1, blocking collectives, on_device(): lax.all_to_all(second_weight, 'ens', split_axis=0, concat_axis=1, tiled=T...  16.3 us
    dot_general x1, matrix products, on_device(): jnp.dot(hidden, own_second[0], preferred_element_type=jnp.float32)  14.9 us
    all_to_all x1, blocking collectives, stacked_exchange(): received = lax.all_to_all(jnp.stack(pieces), axis, 0, 0)  12 us
  transfers between devices with their start and end apart: 2, of which 2 were waited for; matrix products, arithmetic and copies ran while one was open for 1% of the time, Pallas kernels for 0%

profile of v2, /device:TPU:0, one launch (start us, length us, event | category | flops | bytes accessed | tf_op | source)
XLA Modules:
  0.0 187.3 jit_solution(3918088244308441516)
XLA Ops:
  7.2 0.0 copy-start
  7.2 0.0 all-gather.2.cloned.1.call-start
  7.2 1.2 slice_bitcast_fusion.1
  8.4 0.1 pad_maximum_fusion
  8.5 12.0 %all_to_all.14 = bf16[2,1,64,2048]{3,2,1,0:T(8,128)(2,1)S(1)} all-to-all(bf16[2,1,64,2048]{3,2,1,0:T(8,128)(2,1)S(1)} %pad_maximum_fusion), channel_id=1, replica_groups=mesh['dp'=16,'ens'=2] {'ens'}, dimensions={0} | all-to-all | bytes 1048576 | tf_op jit(solution)/shard_map/all_to_all | solution.py:9
  20.5 0.5 copy.8
  21.0 1.0 copy.9
  22.1 0.0 all-gather.2.cloned.1.call-update
  22.1 16.3 %all_to_all.15 = bf16[2,2048,128]{2,1,0:T(8,128)(2,1)S(1)} all-to-all(bf16[2,2048,128]{2,1,0:T(8,128)(2,1)} %param.8), channel_id=1, replica_groups=mesh['dp'=16,'ens'=2] {'ens'}, dimensions={0} | all-to-all | bytes 2097152 | tf_op jit(solution)/shard_map/all_to_all | solution.py:16
  38.4 58.5 %all-gather.2.cloned.1.call-done = bf16[1024,4096]{1,0:T(8,128)(2,1)} async-done(((bf16[64,4096]{1,0:T(8,128)(2,1)}), bf16[1024,4096]{1,0:T(8,128)(2,1)}) %all-gather.2.cloned.1.call-update) | async-done | bytes 8388624 | tf_op jit(solution)/shard_map/all_gather | solution.py:17
  96.9 0.0 copy-done
  96.9 0.0 copy-start.4
  96.9 0.0 copy-start.3
  96.9 14.9 %fusion = f32[768,128]{1,0:T(8,128)S(1)} fusion(bf16[4096,128]{1,0:T(8,128)(2,1)S(1)} %bitcast.26, bf16[1024,4096]{1,0:T(8,128)(2,1)} %all-gather.2.cloned.1.call-done, bf16[768,1024]{1,0:T(8,128)(2,1)S(1)} %copy-done), kind=kOutput, calls=%fused_computation.1 | convolution fusion | flops 7254048768 | bytes 11403264 | tf_op jit(solution)/shard_map/dot_general | solution.py:21
  111.8 0.0 copy-start.1
  111.8 0.5 convolution_reduce_fusion.1
  112.3 0.0 all-reduce.3.cloned.1.call-start
  112.3 0.2 copy-done.1
  112.6 0.5 all-reduce.3.cloned.1.call-update
  113.0 0.0 copy-done.4
  113.1 0.6 convert_multiply_fusion
  113.7 0.6 dynamic_slice.4
  114.9 25.5 %all-reduce.3.cloned.1.call-done = f32[768,128]{1,0:T(8,128)} async-done(((f32[768,128]{1,0:T(8,128)}), f32[768,128]{1,0:T(8,128)}) %all-reduce.3.cloned.1.call-update) | async-done | bytes 393232 | tf_op jit(solution)/shard_map/psum | solution.py:31
  140.4 1.0 broadcast_multiply_fusion
  141.4 0.0 copy-start.2
  141.4 0.5 convolution_reduce_fusion
  141.9 0.0 copy-done.3
  141.9 1.3 multiply_reduce_fusion
  143.2 33.6 %all-reduce = (f32[]{:T(128)}, f32[]{:T(128)}) all-reduce(f32[]{:T(128)} %get-tuple-element.4, f32[]{:T(128)} %get-tuple-element.3), channel_id=1, replica_groups=mesh['dp'=16,'ens'=2] {'dp'}, use_global_device_ids=true, to_apply=%region_2.3 | all-reduce | flops 2 | bytes 16 | tf_op jit(solution)/shard_map/psum | solution.py:30
  178.2 0.0 copy-done.2
Async XLA Ops:
  7.2 89.8 %copy-start = (bf16[768,1024]{1,0:T(8,128)(2,1)S(1)}, bf16[768,1024]{1,0:T(8,128)(2,1)}, u32[]{:S(2)}) copy-start(bf16[768,1024]{1,0:T(8,128)(2,1)} %param.5) | copy-start | bytes 4718596
  7.2 89.7 %all-gather.2.cloned.1.call-start = ((), (), s32[]{:S(2)}) async-start(), calls=%async_computation.2 | async-start | bytes 8912896 | tf_op jit(solution)/shard_map/all_gather | solution.py:17
  96.9 16.1 %copy-start.4 = (s32[2]{0:T(128)S(1)}, s32[2]{0:T(128)}, u32[]{:S(2)}) copy-start(s32[2]{0:T(128)} %param.9) | copy-start | bytes 28
  96.9 44.9 %copy-start.3 = (s32[768]{0:T(1024)S(1)}, s32[768]{0:T(1024)}, u32[]{:S(2)}) copy-start(s32[768]{0:T(1024)} %param.6) | copy-start | bytes 9220
  111.8 0.8 copy-start.1
  112.3 28.1 %all-reduce.3.cloned.1.call-start = ((), (), s32[]{:S(2)}) async-start(), calls=%async_computation.3 | async-start | bytes 786432 | tf_op jit(solution)/shard_map/psum | solution.py:31
  141.4 36.8 %copy-start.2 = (f32[768,128]{1,0:T(8,128)}, f32[768,128]{1,0:T(8,128)S(1)}, u32[]{:S(2)}) copy-start(f32[768,128]{1,0:T(8,128)S(1)} %broadcast_multiply_fusion) | copy-start | bytes 1179652
Sparse Core Ops, SparseCore 0:
  22.2 74.6 all-gather.1
  116.0 24.3 all-reduce.2
